TPU v7x, 512 devices: a whole 4x8x8 slice. The times are simulated.
512 devices in a mesh: expert: 128 (over z, y, core), layer: 4 (over x).
Axes of the slice: x: 4, y: 8, z: 8, core: 2. Of those that a mesh axis runs over, the one named last changes fastest.
Arguments:
- gradient: bfloat16 [512, 256, 1536], P(('layer', 'expert')), parts along dimension 0, may hold values from -80 to 80
- prior_stat: float32 [512, 128], P('layer'), parts along dimension 0, may hold values from -600 to 600, as said below
Outputs:
- update: bfloat16 [512, 256, 1536], P(('layer', 'expert')), parts along dimension 0
- statistic: float32 [512, 128], P('layer'), parts along dimension 0
There are 4 independent parts, one for each index of `layer`. A program takes and returns all parts, laid end to end along the dimension named above; each array names one. Nothing has to cross between parts.
Inputs may be any that keep to these rules, and one draw needn't show every extreme that they name: `prior_stat`: symmetric positive definite.
All inputs are finite; a program needn't handle non-finite values.
Results may differ from a plain program's by a relative error of at most 0.001.
The roundings to bfloat16 on the way count: a program that leaves them out, or rounds other values in their place, can miss the bound.
Values may be sent and summed in bfloat16 or wider, within the bound.
No kernel may reach another device: no remote copies, remote signals or barrier semaphores. Data moves between devices by JAX's collectives and lax.ppermute only.
A program may use at most 64 MiB of HBM per device.

v0:
```python
import jax
import jax.numpy as jnp
from jax import lax
from jax.sharding import Mesh
from jax.sharding import PartitionSpec as P

ITERS = 5
EXPERT = ("expert_0", "expert_1", "expert_2")
LAYER_EXPERT = ("layer", "expert_0", "expert_1", "expert_2")


ridge_rate = 0.001
energy_floor = 1e-06


def split_up(shard, dim, peers):
    dims = shard.shape
    pieces = shard.reshape(*dims[:dim], peers, dims[dim] // peers, *dims[dim + 1 :])
    return jnp.moveaxis(pieces, dim, 0)


def sent_and_summed(shard, axis, dim):
    peers = lax.axis_size(axis)
    pieces = lax.all_to_all(split_up(shard, dim, peers), axis, 0, 0, tiled=True)
    return jnp.sum(pieces, axis=0)


def sum_in_two_steps(shard, axes, dim):
    far, near = axes
    own = sent_and_summed(split_up(shard, dim, lax.axis_size(far)), near, dim + 1)
    return jnp.sum(lax.all_to_all(own, far, 0, 0, tiled=True), axis=0)


def padded_to(lines, peers):
    spare = -len(lines) % peers
    return jnp.pad(lines, [(0, spare)] + [(0, 0)] * (lines.ndim - 1))


def from_everyone(shard, axis):
    copies = jnp.broadcast_to(shard, (lax.axis_size(axis), *shard.shape))
    return lax.all_to_all(copies, axis, split_axis=0, concat_axis=0, tiled=True)


def in_order(pieces, dim):
    dims = list(pieces.shape[1:])
    dims[dim] *= pieces.shape[0]
    return jnp.moveaxis(pieces, 0, dim).reshape(dims)


def gathered_by_axis(shard, axes, dim):
    far, near = axes
    initial = from_everyone(shard, far)
    pieces = jnp.swapaxes(from_everyone(initial, near), 0, 1)
    return in_order(pieces.reshape(-1, *shard.shape), dim)


def nested_sum(shard, axes):
    lines = shard.reshape(-1, shard.shape[-1])
    own = sum_in_two_steps(
        padded_to(lines, lax.axis_size(axes[0]) * lax.axis_size(axes[1])), axes, 0
    )
    whole = gathered_by_axis(own, axes, 0)
    return whole[: len(lines)].reshape(shard.shape)


def matmul_high(left, right):
    return jnp.dot(left, right, precision=lax.Precision.HIGHEST, preferred_element_type=jnp.float32)


def inverse_root(statistic):
    count_rows = statistic.shape[0]
    identity = jnp.eye(count_rows, dtype=jnp.float32)
    ridge_term = ridge_rate * jnp.trace(statistic) / count_rows
    shifted = statistic + ridge_term * identity
    start_scale = 2.5 / jnp.sqrt(jnp.sum(shifted * shifted))
    matrix = start_scale * shifted
    root = start_scale**0.25 * identity
    for repeat in range(ITERS):
        factor = 1.25 * identity - 0.25 * matrix
        root = matmul_high(root, factor)
        square = matmul_high(factor, factor)
        matrix = matmul_high(matmul_high(square, square), matrix)
    return root


def apply_graft(mixed_bf, graft):
    fenced = lax.optimization_barrier(mixed_bf)
    return (graft * fenced.astype(jnp.float32)).astype(jnp.bfloat16)


def slice_grams(pieces):
    grams = jnp.einsum("eqrf,gqrf->eqrg", pieces, pieces, preferred_element_type=jnp.float32)
    return (pieces, grams)


def body(gradient, prior_stat):
    experts = prior_stat.shape[0]
    owners = lax.axis_size(EXPERT)
    local_experts = gradient.shape[0]
    slab_rows = gradient.shape[1]
    width = gradient.shape[2]
    entry_count = slab_rows * width
    slice_rows = slab_rows // owners
    blocked = gradient.reshape(local_experts, owners, slice_rows, width)
    regrouped, row_grams = slice_grams(
        lax.all_to_all(blocked, EXPERT, split_axis=1, concat_axis=0, tiled=True)
    )
    summed = nested_sum(jnp.sum(row_grams, axis=(1, 2)), (("expert_0", "expert_1"), "expert_2"))
    gram_mean = summed / entry_count
    statistic = prior_stat + gram_mean
    root_bf = inverse_root(statistic).astype(jnp.bfloat16)
    flattened = regrouped.reshape(experts, -1)
    products = jnp.dot(root_bf, flattened, preferred_element_type=jnp.float32)
    mixed_bf = products.astype(jnp.bfloat16).reshape(experts, slice_rows, width)
    root_wide = root_bf.astype(jnp.float32)
    update_energy = jnp.sum(matmul_high(root_wide, gram_mean) * root_wide) / experts
    grad_energy = jnp.trace(gram_mean) / experts
    graft = jnp.sqrt((grad_energy + energy_floor) / (update_energy + energy_floor))
    returned = lax.all_to_all(mixed_bf, EXPERT, split_axis=0, concat_axis=1, tiled=True)
    update = apply_graft(returned, graft)
    return (update, statistic)


def solution(mesh):
    torus = Mesh(
        mesh.devices.reshape(8, 8, 2, mesh.shape["layer"]),
        ("expert_0", "expert_1", "expert_2", "layer"),
    )
    return jax.shard_map(
        body,
        mesh=torus,
        in_specs=(P(LAYER_EXPERT, None, None), P("layer", None)),
        out_specs=(P(LAYER_EXPERT, None, None), P("layer", None)),
        check_vma=False,
    )
```

profile of v0, /device:TPU:1, one launch (start us, length us, event | category | flops | bytes accessed | tf_op | source)
XLA Modules:
  0.0 130.4 jit_solution(10027882387608944092)
XLA Ops:
  0.6 2.2 %reshape.61 = bf16[1,128,2,1536]{3,2,1,0:T(2,128)(2,1)S(1)} reshape(bf16[1,256,1536]{2,1,0:T(8,128)(2,1)} %param.2) | data formatting | bytes 1572864 | tf_op jit(solution)/shard_map/reshape | solution.py:104
  2.8 44.2 %all_to_all.44 = bf16[1,128,2,1536]{3,2,0,1:T(2,128)(2,1)S(1)} all-to-all(bf16[1,128,2,1536]{3,2,0,1:T(2,128)(2,1)S(1)} %bitcast.53), channel_id=1, replica_groups=mesh['expert_0'=8,'expert_1'=8,'expert_2'=2,'layer'=4] {'expert_0','expe..., dimensions={1} | all-to-all | bytes 1572864 | tf_op jit(solution)/shard_map/all_to_all | solution.py:106
  47.0 0.1 copy.22
  47.0 0.3 dot_general.67
  47.3 0.4 convolution_bitcast_fusion
  47.7 3.4 %all_to_all.45 = f32[2,64,1,128]{3,1,2,0:T(8,128)S(1)} all-to-all(f32[2,64,1,128]{3,1,2,0:T(8,128)S(1)} %convolution_bitcast_fusion), channel_id=1, replica_groups=mesh['expert_0'=8,'expert_1'=8,'expert_2'=2,'layer'=4] {'expert_2'}, dimensions={0} | all-to-all | bytes 131072 | tf_op jit(solution)/shard_map/all_to_all | solution.py:24
  51.2 15.7 %all_to_all.46 = f32[64,1,128]{2,1,0:T(1,128)S(1)} all-to-all(f32[64,1,128]{2,1,0:T(1,128)S(1)} %bitcast.58), channel_id=1, replica_groups=mesh['expert_0'=8,'expert_1'=8,'expert_2'=2,'layer'=4] {'expert_0','expe..., dimensions={0} | all-to-all | bytes 65536 | tf_op jit(solution)/shard_map/all_to_all | solution.py:31
  66.9 0.1 reduce_sum.60
  66.9 0.6 broadcast_in_dim.13
  67.6 4.6 %all-to-all-start.3 = ((f32[64,1,128]{2,1,0:T(1,128)}), f32[64,1,128]{2,1,0:T(1,128)S(1)}, u32[]{:S(2)}, u32[]{:S(2)}) async-start(f32[64,1,128]{2,1,0:T(1,128)} %broadcast_in_dim.13), calls=%async_computation.3 | async-start | bytes 65536 | tf_op jit(solution)/shard_map/all_to_all | solution.py:41
  72.2 0.0 copy-start.1
  72.2 0.8 copy.13
  73.0 10.0 %all-to-all-done.3 = f32[64,1,128]{2,1,0:T(1,128)S(1)} async-done(((f32[64,1,128]{2,1,0:T(1,128)}), f32[64,1,128]{2,1,0:T(1,128)S(1)}, u32[]{:S(2)}, u32[]{:S(2)}) %all-to-all-start.3) | async-done | bytes 32800 | tf_op jit(solution)/shard_map/all_to_all | solution.py:41
  83.0 6.4 %all_to_all.47 = f32[2,64,1,128]{3,1,2,0:T(8,128)S(1)} all-to-all(f32[2,64,1,128]{3,1,2,0:T(8,128)S(1)} %broadcast_in_dim.14), channel_id=1, replica_groups=mesh['expert_0'=8,'expert_1'=8,'expert_2'=2,'layer'=4] {'expert_2'}, dimensions={0} | all-to-all | bytes 131072 | tf_op jit(solution)/shard_map/all_to_all | solution.py:41
  89.3 0.1 copy.12
  89.4 0.0 copy-done.1
  89.4 0.6 select_reduce_fusion
  90.0 0.0 copy-start
  90.7 0.6 multiply_reduce_fusion
  92.0 0.2 fusion.15
  92.2 0.2 fusion.69
  92.4 0.2 fusion.7
  92.6 0.2 fusion.9
  92.9 0.2 fusion.70
  93.1 0.2 fusion.71
  93.3 0.2 fusion.11
  93.5 0.2 fusion.72
  93.7 0.2 fusion.73
  93.9 0.2 fusion.13
  94.1 0.2 fusion.74
  94.3 0.2 fusion
  94.6 0.0 copy-done
  94.6 0.2 fusion.5
  94.8 0.2 fusion.10
  95.1 0.2 fusion.12
  95.3 0.2 fusion.14
  95.5 0.2 convolution_convert_fusion.1
  95.7 0.4 convolution_convert_fusion
  96.1 1.4 %reshape.64 = bf16[128,2,1536]{2,1,0:T(2,128)(2,1)} reshape(bf16[128,3072]{1,0:T(8,128)(2,1)S(1)} %convolution_convert_fusion) | data formatting | bytes 1572864 | tf_op jit(solution)/shard_map/reshape | solution.py:114
  97.5 5.5 %all-to-all-start.5 = ((bf16[128,2,1536]{2,1,0:T(2,128)(2,1)}), bf16[128,2,1536]{2,1,0:T(2,128)(2,1)S(1)}, u32[]{:S(2)}, u32[]{:S(2)}) async-start(bf16[128,2,1536]{2,1,0:T(2,128)(2,1)} %reshape.64), calls=%async_computation.5 | async-start | bytes 1572864 | tf_op jit(solution)/shard_map/all_to_all | solution.py:119
  103.1 0.9 fusion.4
  104.6 0.8 select_reduce_fusion.1
  106.2 22.9 %all-to-all-done.5 = bf16[128,2,1536]{2,1,0:T(2,128)(2,1)S(1)} async-done(((bf16[128,2,1536]{2,1,0:T(2,128)(2,1)}), bf16[128,2,1536]{2,1,0:T(2,128)(2,1)S(1)}, u32[]{:S(2)}, u32[]{:S(2)}) %all-to-all-start.5) | async-done | bytes 786464 | tf_op jit(solution)/shard_map/all_to_all | solution.py:119
  129.1 0.3 all_to_all.37
  129.4 1.0 multiply_convert_fusion
  (4 shorter events, 0.0 us)
Async XLA Ops:
  67.6 15.4 %all-to-all-start.3 = ((f32[64,1,128]{2,1,0:T(1,128)}), f32[64,1,128]{2,1,0:T(1,128)S(1)}, u32[]{:S(2)}, u32[]{:S(2)}) async-start(f32[64,1,128]{2,1,0:T(1,128)} %broadcast_in_dim.13), calls=%async_computation.3 | async-start | bytes 65536 | tf_op jit(solution)/shard_map/all_to_all | solution.py:41
  72.2 17.2 %copy-start.1 = (f32[128,128]{1,0:T(8,128)S(1)}, f32[128,128]{1,0:T(8,128)}, u32[]{:S(2)}) copy-start(f32[128,128]{1,0:T(8,128)} %param.3) | copy-start | bytes 196612
  90.0 4.6 %copy-start = (f32[128,128]{1,0:T(8,128)}, f32[128,128]{1,0:T(8,128)S(1)}, u32[]{:S(2)}) copy-start(f32[128,128]{1,0:T(8,128)S(1)} %get-tuple-element.3) | copy-start | bytes 196612
  97.5 31.6 %all-to-all-start.5 = ((bf16[128,2,1536]{2,1,0:T(2,128)(2,1)}), bf16[128,2,1536]{2,1,0:T(2,128)(2,1)S(1)}, u32[]{:S(2)}, u32[]{:S(2)}) async-start(bf16[128,2,1536]{2,1,0:T(2,128)(2,1)} %reshape.64), calls=%async_computation.5 | async-start | bytes 1572864 | tf_op jit(solution)/shard_map/all_to_all | solution.py:119
where the time goes:
time: 131 us; the launch traced here: 130 us
  blocking collectives  69.6 us (53%)
  waiting for transfers between devices  32.9 us (25%)
  starting transfers between devices  10.1 us (8%)
  local copies, waits for them, and re-layouts  5.77 us (4%)
  matrix products  5.11 us (4%)
  between operations  3.74 us (3%)
  other arithmetic  3.12 us (2%)
    all_to_all x1, blocking collectives, body(): lax.all_to_all(blocked, EXPERT, split_axis=1, concat_axis=0, tiled=True)  44.2 us
    all_to_all x1, waiting for transfers between devices, body(): lax.all_to_all(mixed_bf, EXPERT, split_axis=0, concat_axis=1, tiled=True)  22.9 us
    all_to_all x1, blocking collectives, sum_in_two_steps(): return jnp.sum(lax.all_to_all(own, far, 0, 0, tiled=True), axis=0)  15.7 us
    all_to_all x1, waiting for transfers between devices, from_everyone(): return lax.all_to_all(copies, axis, split_axis=0, concat_axis=0, tiled=True)  9.99 us
    all_to_all x1, blocking collectives, from_everyone(): return lax.all_to_all(copies, axis, split_axis=0, concat_axis=0, tiled=True)  6.36 us
    all_to_all x1, starting transfers between devices, body(): lax.all_to_all(mixed_bf, EXPERT, split_axis=0, concat_axis=1, tiled=True)  5.53 us
    all_to_all x1, starting transfers between devices, from_everyone(): return lax.all_to_all(copies, axis, split_axis=0, concat_axis=0, tiled=True)  4.59 us
    dot_general x18, matrix products, matmul_high(): jnp.dot(left, right, precision=lax.Precision.HIGHEST, preferred_element_t...  4.37 us
  transfers between devices with their start and end apart: 2, of which 2 were waited for; matrix products, arithmetic and copies ran while one was open for 2% of the time, Pallas kernels for 0%

commit v1 on v0

v1 whole, which is shorter than its diff:
```python
import jax
import jax.numpy as jnp
from jax import lax
from jax.experimental import pallas as pl
from jax.experimental.pallas import tpu as pltpu
from jax.sharding import Mesh
from jax.sharding import PartitionSpec as P

ITERS = 5
AXES = ("z4", "z2", "z1", "y4", "y2", "y1", "core")
LAYER_EXPERT = ("layer",) + AXES
NEAR = ("z1", "y1", "core")
FAR = ("z4", "z2", "y4", "y2")

ridge_rate = 0.001
energy_floor = 1e-06

VMEM = pl.BlockSpec(memory_space=pltpu.VMEM)


def matmul_high(left, right):
    return jnp.dot(left, right, precision=lax.Precision.HIGHEST, preferred_element_type=jnp.float32)


def peers_of(axes):
    peers = 1
    for axis in axes:
        peers *= lax.axis_size(axis)
    return peers


def exchanged(pieces, axes):
    return lax.all_to_all(pieces, axes, split_axis=0, concat_axis=0, tiled=True)


def from_everyone(shard, axes):
    return exchanged(jnp.broadcast_to(shard[None], (peers_of(axes), *shard.shape)), axes)


def summed_over_all(gram):
    rows, width = gram.shape
    near = peers_of(NEAR)
    own = jnp.sum(exchanged(gram.reshape(near, rows // near, width), NEAR), axis=0)
    own = jnp.sum(from_everyone(own, FAR), axis=0)
    return from_everyone(own, NEAR).reshape(rows, width)


def whole_sum(array):
    return jnp.sum(jnp.sum(array, axis=0, keepdims=True), axis=1, keepdims=True)


def root_and_products(entry_count, gram_sum, prior_stat, flattened):
    experts = prior_stat.shape[0]
    rows = 8
    width = flattened.shape[1] // rows
    lanes = 128
    tiles = width // lanes

    def kernel(gram_ref, prior_ref, flat_ref, stat_ref, root_ref, mixed_ref, wide_ref):
        shape = (experts, experts)
        diagonal = lax.broadcasted_iota(jnp.int32, shape, 0) == lax.broadcasted_iota(jnp.int32, shape, 1)
        statistic = prior_ref[...] + gram_ref[...] * (1.0 / entry_count)
        stat_ref[...] = statistic
        ridge = whole_sum(jnp.where(diagonal, statistic, 0.0)) * (ridge_rate / experts)
        shifted = statistic + jnp.where(diagonal, ridge, 0.0)
        start = 2.5 / jnp.sqrt(whole_sum(shifted * shifted))
        scaled_identity = jnp.where(diagonal, 1.25, 0.0)
        matrix = start * shifted
        factor = scaled_identity - 0.25 * matrix
        root = jnp.sqrt(jnp.sqrt(start)) * factor
        for repeat in range(ITERS - 1):
            square = matmul_high(factor, factor)
            matrix = matmul_high(matmul_high(square, square), matrix)
            factor = scaled_identity - 0.25 * matrix
            root = matmul_high(root, factor)
        root_bf = root.astype(jnp.bfloat16)
        root_ref[...] = root_bf
        for row in range(rows):
            part = jnp.dot(root_bf, flat_ref[:, row * width : (row + 1) * width], preferred_element_type=jnp.float32)
            for tile in range(tiles):
                wide_ref[tile, pl.ds(row, experts, stride=rows), :] = part[:, tile * lanes : (tile + 1) * lanes]
        for tile in range(tiles):
            mixed_ref[:, :, tile * lanes : (tile + 1) * lanes] = (
                wide_ref[tile].reshape(experts, rows, lanes).astype(jnp.bfloat16)
            )

    return pl.pallas_call(
        kernel,
        out_shape=(
            jax.ShapeDtypeStruct((experts, experts), jnp.float32),
            jax.ShapeDtypeStruct((experts, experts), jnp.bfloat16),
            jax.ShapeDtypeStruct((experts, rows, width), jnp.bfloat16),
        ),
        in_specs=[VMEM] * 3,
        out_specs=(VMEM,) * 3,
        scratch_shapes=[pltpu.VMEM((tiles, experts * rows, lanes), jnp.float32)],
        name="root_and_products",
    )(gram_sum, prior_stat, flattened)


def body(gradient, prior_stat):
    experts = prior_stat.shape[0]
    slab_rows, width = gradient.shape[1:]
    entry_count = slab_rows * width
    rows = 8
    blocks = slab_rows // rows
    columns = experts // blocks
    piece = width // columns
    pieces = gradient.reshape(blocks, rows, columns, piece).transpose(0, 2, 1, 3).reshape(experts, rows, piece)
    regrouped = exchanged(pieces, AXES)
    flattened = regrouped.reshape(experts, rows * piece)
    gram = jnp.einsum("ek,gk->eg", flattened, flattened, preferred_element_type=jnp.float32)
    gram_sum = summed_over_all(gram)
    statistic, root_bf, mixed_bf = root_and_products(entry_count, gram_sum, prior_stat, flattened)
    returned = exchanged(mixed_bf, AXES)
    gram_mean = gram_sum / entry_count
    root_wide = root_bf.astype(jnp.float32)
    update_energy = jnp.sum(matmul_high(root_wide, gram_mean) * root_wide) / experts
    grad_energy = jnp.trace(gram_mean) / experts
    graft = jnp.sqrt((grad_energy + energy_floor) / (update_energy + energy_floor))
    update = (graft * returned.astype(jnp.float32)).astype(jnp.bfloat16)
    update = update.reshape(blocks, columns, rows, piece).transpose(0, 2, 1, 3).reshape(gradient.shape)
    return (update, statistic)


def solution(mesh):
    torus = Mesh(
        mesh.devices.reshape(2, 2, 2, 2, 2, 2, 2, mesh.shape["layer"]),
        AXES + ("layer",),
    )
    return jax.shard_map(
        body,
        mesh=torus,
        in_specs=(P(LAYER_EXPERT, None, None), P("layer", None)),
        out_specs=(P(LAYER_EXPERT, None, None), P("layer", None)),
        check_vma=False,
    )
```

time: 131 us -> 119 us (0.908)
  waiting for transfers between devices: 32.9 us -> 26.3 us
  Pallas kernels: 0 us -> 5.82 us
  matrix products: 5.11 us -> 1.15 us
  local copies, waits for them, and re-layouts: 5.77 us -> 3 us
  blocking collectives: 69.6 us -> 66.9 us
  between operations: 3.74 us -> 2.09 us
  starting transfers between devices: 10.1 us -> 11.7 us
  other arithmetic: 3.12 us -> 1.75 us
    all_to_all x2, waiting for transfers between devices: 32.9 us -> 26.3 us  [exchanged(): return lax.all_to_all(pieces, axes, split_axis=0, concat_axis=0, tiled=True)]
    pallas_call x0 -> x1, Pallas kernels: none -> 5.82 us  [root_and_products(): pl.pallas_call(kernel, out_shape=(jax.ShapeDtypeStruct((experts, experts)...]
    dot_general x18 -> x1, matrix products: 4.37 us -> 0.78 us  [matmul_high(): jnp.dot(left, right, precision=lax.Precision.HIGHEST, preferred_element_t...]
    reshape x2 -> x1, local copies, waits for them, and re-layouts: 3.61 us -> 0.36 us  [body(): flattened = regrouped.reshape(experts, rows * piece)]
    all_to_all x4 -> x3, blocking collectives: 69.6 us -> 66.9 us  [exchanged(): return lax.all_to_all(pieces, axes, split_axis=0, concat_axis=0, tiled=True)]
    unnamed x4 -> x7, local copies, waits for them, and re-layouts: 0.01 us -> 1.64 us
    all_to_all x2, starting transfers between devices: 10.1 us -> 11.7 us  [exchanged(): return lax.all_to_all(pieces, axes, split_axis=0, concat_axis=0, tiled=True)]
where the time goes in v1:
time: 119 us
  blocking collectives  66.9 us (56%)
  waiting for transfers between devices  26.3 us (22%)
  starting transfers between devices  11.7 us (10%)
  Pallas kernels  5.82 us (5%)
  local copies, waits for them, and re-layouts  3 us (3%)
  between operations  2.09 us (2%)
  other arithmetic  1.75 us (1%)
    all_to_all x3, blocking collectives, exchanged(): return lax.all_to_all(pieces, axes, split_axis=0, concat_axis=0, tiled=True)  66.9 us
    all_to_all x2, waiting for transfers between devices, exchanged(): return lax.all_to_all(pieces, axes, split_axis=0, concat_axis=0, tiled=True)  26.3 us
    all_to_all x2, starting transfers between devices, exchanged(): return lax.all_to_all(pieces, axes, split_axis=0, concat_axis=0, tiled=True)  11.7 us
    pallas_call x1, Pallas kernels, root_and_products(): pl.pallas_call(kernel, out_shape=(jax.ShapeDtypeStruct((experts, experts)...  5.82 us
  transfers between devices with their start and end apart: 2, of which 2 were waited for; matrix products, arithmetic and copies ran while one was open for 2% of the time, Pallas kernels for 0%

profile of v1, /device:TPU:1, one launch (start us, length us, event | category | flops | bytes accessed | tf_op | source)
XLA Modules:
  0.0 118.8 jit_solution(6580861105443640037)
XLA Ops:
  0.6 44.4 %all_to_all.25 = bf16[128,8,384]{2,1,0:T(8,128)(2,1)S(1)} all-to-all(bf16[128,8,384]{2,1,0:T(8,128)(2,1)} %bitcast.20), channel_id=1, replica_groups=mesh['z4'=2,'z2'=2,'z1'=2,'y4'=2,'y2'=2,'y1'=2,'core'=2,'layer'=4] {'z4'..., dimensions={0} | all-to-all | bytes 1572864 | tf_op jit(solution)/shard_map/all_to_all | solution.py:33
  45.0 0.4 dot_general.8
  45.4 0.4 reshape.43
  45.7 0.4 fusion.4
  46.1 7.2 %all_to_all.26 = f32[8,16,128]{2,1,0:T(8,128)S(1)} all-to-all(f32[8,16,128]{2,1,0:T(8,128)S(1)} %fusion.4), channel_id=1, replica_groups=mesh['z4'=2,'z2'=2,'z1'=2,'y4'=2,'y2'=2,'y1'=2,'core'=2,'layer'=4] {'z1'..., dimensions={0} | all-to-all | bytes 131072 | tf_op jit(solution)/shard_map/all_to_all | solution.py:33
  53.3 15.3 %all_to_all.27 = f32[16,16,128]{2,1,0:T(8,128)S(1)} all-to-all(f32[16,16,128]{2,1,0:T(8,128)S(1)} %broadcast_in_dim.7), channel_id=1, replica_groups=mesh['z4'=2,'z2'=2,'z1'=2,'y4'=2,'y2'=2,'y1'=2,'core'=2,'layer'=4] {'z4'..., dimensions={0} | all-to-all | bytes 262144 | tf_op jit(solution)/shard_map/all_to_all | solution.py:33
  68.7 0.6 broadcast_in_dim.8
  69.3 5.5 %all-to-all-start.3 = ((f32[8,16,128]{2,1,0:T(8,128)}), f32[8,16,128]{2,1,0:T(8,128)S(1)}, u32[]{:S(2)}, u32[]{:S(2)}) async-start(f32[8,16,128]{2,1,0:T(8,128)} %broadcast_in_dim.8), calls=%async_computation.3 | async-start | bytes 131072 | tf_op jit(solution)/shard_map/all_to_all | solution.py:33
  74.8 1.0 copy.4
  75.9 3.2 %all-to-all-done.3 = f32[8,16,128]{2,1,0:T(8,128)S(1)} async-done(((f32[8,16,128]{2,1,0:T(8,128)}), f32[8,16,128]{2,1,0:T(8,128)S(1)}, u32[]{:S(2)}, u32[]{:S(2)}) %all-to-all-start.3) | async-done | bytes 65568 | tf_op jit(solution)/shard_map/all_to_all | solution.py:33
  79.0 0.0 copy-start
  79.0 0.6 copy-done
  79.7 5.8 %root_and_products.1 = (f32[128,128]{1,0:T(8,128)}, bf16[128,128]{1,0:T(8,128)(2,1)}, bf16[128,8,384]{2,1,0:T(8,128)(2,1)}) custom-call(f32[128,128]{1,0:T(8,128)} %bitcast.18, f32[128,128]{1,0:T(8,128)} %prior_ref.1, bf16[128,3072]{1,0:T(8,128)(2,1)} %bitcast.17), custom_call_target="tpu_custom_call" | custom-call | tf_op jit(solution)/shard_map/root_and_products/pallas_call | solution.py:87
  85.5 0.0 copy-start.1
  85.5 0.0 copy-start.2
  85.5 6.2 %all-to-all-start.4 = ((bf16[128,8,384]{2,1,0:T(8,128)(2,1)}), bf16[128,8,384]{2,1,0:T(8,128)(2,1)S(1)}, u32[]{:S(2)}, u32[]{:S(2)}) async-start(bf16[128,8,384]{2,1,0:T(8,128)(2,1)} %get-tuple-element.6), calls=%async_computation.4 | async-start | bytes 1572864 | tf_op jit(solution)/shard_map/all_to_all | solution.py:33
  91.7 0.0 copy-done.1
  91.7 0.0 copy-done.2
  91.7 0.8 fusion
  93.1 0.7 select_reduce_fusion
  94.6 23.2 %all-to-all-done.4 = bf16[128,8,384]{2,1,0:T(8,128)(2,1)S(1)} async-done(((bf16[128,8,384]{2,1,0:T(8,128)(2,1)}), bf16[128,8,384]{2,1,0:T(8,128)(2,1)S(1)}, u32[]{:S(2)}, u32[]{:S(2)}) %all-to-all-start.4) | async-done | bytes 786464 | tf_op jit(solution)/shard_map/all_to_all | solution.py:33
  117.7 1.0 multiply_convert_fusion
  (4 shorter events, 0.0 us)
Async XLA Ops:
  69.3 9.7 %all-to-all-start.3 = ((f32[8,16,128]{2,1,0:T(8,128)}), f32[8,16,128]{2,1,0:T(8,128)S(1)}, u32[]{:S(2)}, u32[]{:S(2)}) async-start(f32[8,16,128]{2,1,0:T(8,128)} %broadcast_in_dim.8), calls=%async_computation.3 | async-start | bytes 131072 | tf_op jit(solution)/shard_map/all_to_all | solution.py:33
  79.0 0.6 copy-start
  85.5 6.2 %copy-start.1 = (f32[8,16,128]{2,1,0:T(8,128)S(1)}, f32[8,16,128]{2,1,0:T(8,128)}, u32[]{:S(2)}) copy-start(f32[8,16,128]{2,1,0:T(8,128)} %copy-done) | copy-start | bytes 196612
  85.5 6.2 %copy-start.2 = (bf16[128,128]{1,0:T(8,128)(2,1)S(1)}, bf16[128,128]{1,0:T(8,128)(2,1)}, u32[]{:S(2)}) copy-start(bf16[128,128]{1,0:T(8,128)(2,1)} %get-tuple-element.5) | copy-start | bytes 98308
  85.5 32.2 %all-to-all-start.4 = ((bf16[128,8,384]{2,1,0:T(8,128)(2,1)}), bf16[128,8,384]{2,1,0:T(8,128)(2,1)S(1)}, u32[]{:S(2)}, u32[]{:S(2)}) async-start(bf16[128,8,384]{2,1,0:T(8,128)(2,1)} %get-tuple-element.6), calls=%async_computation.4 | async-start | bytes 1572864 | tf_op jit(solution)/shard_map/all_to_all | solution.py:33

commit v2 on v1

v2 whole, which is shorter than its diff:
```python
import jax
import jax.numpy as jnp
from jax import lax
from jax.experimental import pallas as pl
from jax.experimental.pallas import tpu as pltpu
from jax.sharding import Mesh
from jax.sharding import PartitionSpec as P

ITERS = 5
AXES = ("z4", "z2", "z1", "y4", "y2", "y1", "core")
LAYER_EXPERT = ("layer",) + AXES
NEAR = ("z1", "y1", "core")
FAR = ("z4", "z2", "y4", "y2")

ridge_rate = 0.001
energy_floor = 1e-06

ROWS = 8
LANES = 128

VMEM = pl.BlockSpec(memory_space=pltpu.VMEM)


def matmul_high(left, right):
    return jnp.dot(left, right, precision=lax.Precision.HIGHEST, preferred_element_type=jnp.float32)


def peers_of(axes):
    peers = 1
    for axis in axes:
        peers *= lax.axis_size(axis)
    return peers


def exchanged(pieces, axes):
    return lax.all_to_all(pieces, axes, split_axis=0, concat_axis=0, tiled=True)


def from_everyone(shard, axes):
    return exchanged(jnp.broadcast_to(shard[None], (peers_of(axes), *shard.shape)), axes)


def summed_over_all(gram):
    rows, width = gram.shape
    near = peers_of(NEAR)
    own = jnp.sum(exchanged(gram.reshape(near, rows // near, width), NEAR), axis=0)
    own = jnp.sum(from_everyone(own, FAR), axis=0)
    return from_everyone(own, NEAR).reshape(rows, width)


def in_vmem(array):
    return pltpu.with_memory_space_constraint(array, pltpu.VMEM)


def whole_sum(array):
    return jnp.sum(jnp.sum(array, axis=0, keepdims=True), axis=1, keepdims=True)


def widen_rows(pieces_ref, wide_ref):
    for tile in range(wide_ref.shape[0]):
        lanes = pieces_ref[:, :, tile * LANES : (tile + 1) * LANES]
        wide_ref[tile] = lanes.astype(jnp.float32).reshape(wide_ref.shape[1:])


def one_row(wide_ref, row, experts, rows):
    parts = [wide_ref[tile, pl.ds(row, experts, stride=rows), :] for tile in range(wide_ref.shape[0])]
    return jnp.concatenate(parts, axis=1).astype(jnp.bfloat16)


def wide_scratch(experts, rows, width):
    return pltpu.VMEM((width // LANES, experts * rows, LANES), jnp.float32)


def piece_gram(pieces):
    experts, rows, width = pieces.shape

    def kernel(pieces_ref, gram_ref, wide_ref):
        widen_rows(pieces_ref, wide_ref)
        gram = jnp.zeros((experts, experts), jnp.float32)
        for row in range(rows):
            line = one_row(wide_ref, row, experts, rows)
            gram += lax.dot_general(line, line, (((1,), (1,)), ((), ())), preferred_element_type=jnp.float32)
        gram_ref[...] = gram

    return pl.pallas_call(
        kernel,
        out_shape=pltpu.VMEM((experts, experts), jnp.float32),
        in_specs=[VMEM],
        out_specs=VMEM,
        scratch_shapes=[wide_scratch(experts, rows, width)],
        name="piece_gram",
    )(in_vmem(pieces))


def grafted_products(entry_count, gram_sum, prior_stat, pieces):
    experts, rows, width = pieces.shape

    def kernel(gram_ref, prior_ref, pieces_ref, stat_ref, update_ref, wide_ref, out_ref):
        widen_rows(pieces_ref, wide_ref)
        shape = (experts, experts)
        diagonal = lax.broadcasted_iota(jnp.int32, shape, 0) == lax.broadcasted_iota(jnp.int32, shape, 1)
        gram_mean = gram_ref[...] * (1.0 / entry_count)
        statistic = prior_ref[...] + gram_mean
        stat_ref[...] = statistic
        ridge = whole_sum(jnp.where(diagonal, statistic, 0.0)) * (ridge_rate / experts)
        shifted = statistic + jnp.where(diagonal, ridge, 0.0)
        start = 2.5 / jnp.sqrt(whole_sum(shifted * shifted))
        scaled_identity = jnp.where(diagonal, 1.25, 0.0)
        matrix = start * shifted
        factor = scaled_identity - 0.25 * matrix
        root = jnp.sqrt(jnp.sqrt(start)) * factor
        for repeat in range(ITERS - 1):
            square = matmul_high(factor, factor)
            matrix = matmul_high(matmul_high(square, square), matrix)
            factor = scaled_identity - 0.25 * matrix
            root = matmul_high(root, factor)
        root_bf = root.astype(jnp.bfloat16)
        root_wide = root_bf.astype(jnp.float32)
        update_energy = whole_sum(matmul_high(root_wide, gram_mean) * root_wide) / experts
        grad_energy = whole_sum(jnp.where(diagonal, gram_mean, 0.0)) / experts
        graft = jnp.sqrt((grad_energy + energy_floor) / (update_energy + energy_floor))
        for row in range(rows):
            line = one_row(wide_ref, row, experts, rows)
            mixed_bf = jnp.dot(root_bf, line, preferred_element_type=jnp.float32).astype(jnp.bfloat16)
            update = graft * mixed_bf.astype(jnp.float32)
            for tile in range(width // LANES):
                out_ref[tile, pl.ds(row, experts, stride=rows), :] = update[:, tile * LANES : (tile + 1) * LANES]
        for tile in range(width // LANES):
            update_ref[:, :, tile * LANES : (tile + 1) * LANES] = (
                out_ref[tile].reshape(experts, rows, LANES).astype(jnp.bfloat16)
            )

    return pl.pallas_call(
        kernel,
        out_shape=(
            pltpu.VMEM((experts, experts), jnp.float32),
            pltpu.VMEM(pieces.shape, jnp.bfloat16),
        ),
        in_specs=[VMEM] * 3,
        out_specs=(VMEM,) * 2,
        scratch_shapes=[wide_scratch(experts, rows, width)] * 2,
        name="grafted_products",
    )(in_vmem(gram_sum), in_vmem(prior_stat), in_vmem(pieces))


def body(gradient, prior_stat):
    experts = prior_stat.shape[0]
    slab_rows, width = gradient.shape[1:]
    blocks = slab_rows // ROWS
    columns = experts // blocks
    piece = width // columns
    pieces = gradient.reshape(blocks, ROWS, columns, piece).transpose(0, 2, 1, 3).reshape(experts, ROWS, piece)
    regrouped = exchanged(pieces, AXES)
    gram_sum = summed_over_all(piece_gram(regrouped))
    statistic, scaled = grafted_products(slab_rows * width, gram_sum, prior_stat, regrouped)
    returned = exchanged(scaled, AXES)
    update = returned.reshape(blocks, columns, ROWS, piece).transpose(0, 2, 1, 3).reshape(gradient.shape)
    return (update, statistic)


def solution(mesh):
    torus = Mesh(
        mesh.devices.reshape(2, 2, 2, 2, 2, 2, 2, mesh.shape["layer"]),
        AXES + ("layer",),
    )
    return jax.shard_map(
        body,
        mesh=torus,
        in_specs=(P(LAYER_EXPERT, None, None), P("layer", None)),
        out_specs=(P(LAYER_EXPERT, None, None), P("layer", None)),
        check_vma=False,
    )
```

time: 119 us -> 116 us (0.975)
  blocking collectives: 66.9 us -> 75.8 us
  starting transfers between devices: 11.7 us -> 6.05 us
  other arithmetic: 1.75 us -> 0.03 us
  local copies, waits for them, and re-layouts: 3 us -> 1.53 us
  between operations: 2.09 us -> 0.68 us
    all_to_all x3 -> x4, blocking collectives: 66.9 us -> 75.8 us  [exchanged(): return lax.all_to_all(pieces, axes, split_axis=0, concat_axis=0, tiled=True)]
    all_to_all x2 -> x1, starting transfers between devices: 11.7 us -> 6.05 us  [exchanged(): return lax.all_to_all(pieces, axes, split_axis=0, concat_axis=0, tiled=True)]
    all_to_all x2 -> x1, waiting for transfers between devices: 26.3 us -> 25.4 us  [exchanged(): return lax.all_to_all(pieces, axes, split_axis=0, concat_axis=0, tiled=True)]
    pallas_call x1 -> x2, Pallas kernels: 5.82 us -> 5.57 us  [the longest x1 4.94 us: grafted_products(): pl.pallas_call(kernel, out_shape=(pltpu.VMEM((experts, experts), jnp.floa...]
  transfers between devices with their start and end apart: 2 -> 1, of which waited for: 2 -> 1; matrix products, arithmetic and copies ran while one was open for 2% -> 1% of each run, Pallas kernels for 0% -> 0%
where the time goes in v2:
time: 116 us; the launch traced here: 115 us
  blocking collectives  75.8 us (65%)
  waiting for transfers between devices  25.4 us (22%)
  starting transfers between devices  6.05 us (5%)
  Pallas kernels  5.57 us (5%)
  local copies, waits for them, and re-layouts  1.53 us (1%)
    all_to_all x4, blocking collectives, exchanged(): return lax.all_to_all(pieces, axes, split_axis=0, concat_axis=0, tiled=True)  75.8 us
    all_to_all x1, waiting for transfers between devices, exchanged(): return lax.all_to_all(pieces, axes, split_axis=0, concat_axis=0, tiled=True)  25.4 us
    all_to_all x1, starting transfers between devices, exchanged(): return lax.all_to_all(pieces, axes, split_axis=0, concat_axis=0, tiled=True)  6.05 us
    pallas_call x1, Pallas kernels, grafted_products(): pl.pallas_call(kernel, out_shape=(pltpu.VMEM((experts, experts), jnp.floa...  4.94 us
  transfers between devices with their start and end apart: 1, of which 1 were waited for; matrix products, arithmetic and copies ran while one was open for 1% of the time, Pallas kernels for 0%

profile of v2, /device:TPU:1, one launch (start us, length us, event | category | flops | bytes accessed | tf_op | source)
XLA Modules:
  0.0 115.1 jit_solution(1182531661444401074)
XLA Ops:
  0.6 44.4 %all_to_all.25.pieces_ref = bf16[128,8,384]{2,1,0:T(8,128)(2,1)S(1)} all-to-all(bf16[128,8,384]{2,1,0:T(8,128)(2,1)} %bitcast.15), channel_id=1, replica_groups=mesh['z4'=2,'z2'=2,'z1'=2,'y4'=2,'y2'=2,'y1'=2,'core'=2,'layer'=4] {'z4'..., dimensions={0} | all-to-all | bytes 1572864 | tf_op jit(solution)/shard_map/all_to_all | solution.py:36
  45.0 0.6 piece_gram.1
  45.6 7.2 %all_to_all.26 = f32[8,16,128]{2,1,0:T(8,128)S(1)} all-to-all(f32[8,16,128]{2,1,0:T(8,128)S(1)} %bitcast.13), channel_id=1, replica_groups=mesh['z4'=2,'z2'=2,'z1'=2,'y4'=2,'y2'=2,'y1'=2,'core'=2,'layer'=4] {'z1'..., dimensions={0} | all-to-all | bytes 131072 | tf_op jit(solution)/shard_map/all_to_all | solution.py:36
  52.8 15.4 %all_to_all.27 = f32[16,16,128]{2,1,0:T(8,128)S(1)} all-to-all(f32[16,16,128]{2,1,0:T(8,128)S(1)} %broadcast_in_dim.4), channel_id=1, replica_groups=mesh['z4'=2,'z2'=2,'z1'=2,'y4'=2,'y2'=2,'y1'=2,'core'=2,'layer'=4] {'z4'..., dimensions={0} | all-to-all | bytes 262144 | tf_op jit(solution)/shard_map/all_to_all | solution.py:36
  68.2 0.0 copy-start
  68.2 8.9 %all_to_all.28 = f32[8,16,128]{2,1,0:T(8,128)S(1)} all-to-all(f32[8,16,128]{2,1,0:T(8,128)S(1)} %broadcast_in_dim.5), channel_id=1, replica_groups=mesh['z4'=2,'z2'=2,'z1'=2,'y4'=2,'y2'=2,'y1'=2,'core'=2,'layer'=4] {'z1'..., dimensions={0} | all-to-all | bytes 131072 | tf_op jit(solution)/shard_map/all_to_all | solution.py:36
  77.2 0.0 copy-done
  77.2 4.9 %grafted_products.1 = (f32[128,128]{1,0:T(8,128)S(1)}, bf16[128,8,384]{2,1,0:T(8,128)(2,1)}) custom-call(f32[128,128]{1,0:T(8,128)S(1)} %bitcast.12, f32[128,128]{1,0:T(8,128)S(1)} %copy-done, bf16[128,8,384]{2,1,0:T(8,128)(2,1)S(1)} %all_to_all.25.pieces_ref), custom_call_target="tpu_custom_call" | custom-call | tf_op jit(solution)/shard_map/grafted_products/pallas_call | solution.py:133
  82.1 6.1 %all-to-all-start.4 = ((bf16[128,8,384]{2,1,0:T(8,128)(2,1)}), bf16[128,8,384]{2,1,0:T(8,128)(2,1)S(1)}, u32[]{:S(2)}, u32[]{:S(2)}) async-start(bf16[128,8,384]{2,1,0:T(8,128)(2,1)} %get-tuple-element.4), calls=%async_computation.4 | async-start | bytes 1572864 | tf_op jit(solution)/shard_map/all_to_all | solution.py:36
  88.2 0.6 copy.5
  88.8 25.4 %all-to-all-done.4 = bf16[128,8,384]{2,1,0:T(8,128)(2,1)S(1)} async-done(((bf16[128,8,384]{2,1,0:T(8,128)(2,1)}), bf16[128,8,384]{2,1,0:T(8,128)(2,1)S(1)}, u32[]{:S(2)}, u32[]{:S(2)}) %all-to-all-start.4) | async-done | bytes 786464 | tf_op jit(solution)/shard_map/all_to_all | solution.py:36
  114.2 0.9 copy.6
  (4 shorter events, 0.0 us)
Async XLA Ops:
  68.2 9.0 %copy-start = (f32[128,128]{1,0:T(8,128)S(1)}, f32[128,128]{1,0:T(8,128)}, u32[]{:S(2)}) copy-start(f32[128,128]{1,0:T(8,128)} %prior_ref.1) | copy-start | bytes 196612
  82.1 32.1 %all-to-all-start.4 = ((bf16[128,8,384]{2,1,0:T(8,128)(2,1)}), bf16[128,8,384]{2,1,0:T(8,128)(2,1)S(1)}, u32[]{:S(2)}, u32[]{:S(2)}) async-start(bf16[128,8,384]{2,1,0:T(8,128)(2,1)} %get-tuple-element.4), calls=%async_computation.4 | async-start | bytes 1572864 | tf_op jit(solution)/shard_map/all_to_all | solution.py:36

commit v3 on v2

--- a/solution.py
+++ b/solution.py
@@ -95,13 +95,15 @@
 def grafted_products(entry_count, gram_sum, prior_stat, pieces):
     experts, rows, width = pieces.shape
 
-    def kernel(gram_ref, prior_ref, pieces_ref, stat_ref, update_ref, wide_ref, out_ref):
+    def kernel(gram_ref, prior_ref, pieces_ref, stat_ref, update_ref, wide_ref, out_ref, held_ref, arrival):
         widen_rows(pieces_ref, wide_ref)
         shape = (experts, experts)
         diagonal = lax.broadcasted_iota(jnp.int32, shape, 0) == lax.broadcasted_iota(jnp.int32, shape, 1)
         gram_mean = gram_ref[...] * (1.0 / entry_count)
         statistic = prior_ref[...] + gram_mean
-        stat_ref[...] = statistic
+        held_ref[...] = statistic
+        written = pltpu.make_async_copy(held_ref, stat_ref, arrival)
+        written.start()
         ridge = whole_sum(jnp.where(diagonal, statistic, 0.0)) * (ridge_rate / experts)
         shifted = statistic + jnp.where(diagonal, ridge, 0.0)
         start = 2.5 / jnp.sqrt(whole_sum(shifted * shifted))
@@ -129,16 +131,22 @@
             update_ref[:, :, tile * LANES : (tile + 1) * LANES] = (
                 out_ref[tile].reshape(experts, rows, LANES).astype(jnp.bfloat16)
             )
+        written.wait()
 
     return pl.pallas_call(
         kernel,
         out_shape=(
-            pltpu.VMEM((experts, experts), jnp.float32),
+            pltpu.HBM((experts, experts), jnp.float32),
             pltpu.VMEM(pieces.shape, jnp.bfloat16),
         ),
         in_specs=[VMEM] * 3,
-        out_specs=(VMEM,) * 2,
-        scratch_shapes=[wide_scratch(experts, rows, width)] * 2,
+        out_specs=(pl.BlockSpec(memory_space=pltpu.HBM), VMEM),
+        scratch_shapes=[
+            wide_scratch(experts, rows, width),
+            wide_scratch(experts, rows, width),
+            pltpu.VMEM((experts, experts), jnp.float32),
+            pltpu.SemaphoreType.DMA,
+        ],
         name="grafted_products",
     )(in_vmem(gram_sum), in_vmem(prior_stat), in_vmem(pieces))
 

time: 116 us -> 114 us (0.983)
  blocking collectives: 75.8 us -> 107 us
  waiting for transfers between devices: 25.4 us -> 0 us
  starting transfers between devices: 6.05 us -> 0 us
    all_to_all x4 -> x5, blocking collectives: 75.8 us -> 107 us  [exchanged(): return lax.all_to_all(pieces, axes, split_axis=0, concat_axis=0, tiled=True)]
    all_to_all x1 -> x0, waiting for transfers between devices: 25.4 us -> none  [exchanged(): return lax.all_to_all(pieces, axes, split_axis=0, concat_axis=0, tiled=True)]
    all_to_all x1 -> x0, starting transfers between devices: 6.05 us -> none  [exchanged(): return lax.all_to_all(pieces, axes, split_axis=0, concat_axis=0, tiled=True)]
  transfers between devices with their start and end apart: 1 -> 0, of which waited for: 1 -> 0; matrix products, arithmetic and copies ran while one was open for 1% -> 0% of each run, Pallas kernels for 0% -> 0%
where the time goes in v3:
time: 114 us; the launch traced here: 113 us
  blocking collectives  107 us (94%)
  Pallas kernels  4.55 us (4%)
    all_to_all x5, blocking collectives, exchanged(): return lax.all_to_all(pieces, axes, split_axis=0, concat_axis=0, tiled=True)  107 us
    pallas_call x1, Pallas kernels, grafted_products(): pl.pallas_call(kernel, out_shape=(pltpu.HBM((experts, experts), jnp.float...  3.92 us

profile of v3, /device:TPU:1, one launch (start us, length us, event | category | flops | bytes accessed | tf_op | source)
XLA Modules:
  0.0 113.4 jit_solution(9574726803045303506)
XLA Ops:
  0.6 44.4 %all_to_all.25.pieces_ref = bf16[128,8,384]{2,1,0:T(8,128)(2,1)S(1)} all-to-all(bf16[128,8,384]{2,1,0:T(8,128)(2,1)} %bitcast.15), channel_id=1, replica_groups=mesh['z4'=2,'z2'=2,'z1'=2,'y4'=2,'y2'=2,'y1'=2,'core'=2,'layer'=4] {'z4'..., dimensions={0} | all-to-all | bytes 1572864 | tf_op jit(solution)/shard_map/all_to_all | solution.py:36
  45.0 0.6 piece_gram.1
  45.6 7.2 %all_to_all.26 = f32[8,16,128]{2,1,0:T(8,128)S(1)} all-to-all(f32[8,16,128]{2,1,0:T(8,128)S(1)} %bitcast.13), channel_id=1, replica_groups=mesh['z4'=2,'z2'=2,'z1'=2,'y4'=2,'y2'=2,'y1'=2,'core'=2,'layer'=4] {'z1'..., dimensions={0} | all-to-all | bytes 131072 | tf_op jit(solution)/shard_map/all_to_all | solution.py:36
  52.8 15.4 %all_to_all.27 = f32[16,16,128]{2,1,0:T(8,128)S(1)} all-to-all(f32[16,16,128]{2,1,0:T(8,128)S(1)} %broadcast_in_dim.4), channel_id=1, replica_groups=mesh['z4'=2,'z2'=2,'z1'=2,'y4'=2,'y2'=2,'y1'=2,'core'=2,'layer'=4] {'z4'..., dimensions={0} | all-to-all | bytes 262144 | tf_op jit(solution)/shard_map/all_to_all | solution.py:36
  68.2 0.0 copy-start
  68.2 8.9 %all_to_all.28 = f32[8,16,128]{2,1,0:T(8,128)S(1)} all-to-all(f32[8,16,128]{2,1,0:T(8,128)S(1)} %broadcast_in_dim.5), channel_id=1, replica_groups=mesh['z4'=2,'z2'=2,'z1'=2,'y4'=2,'y2'=2,'y1'=2,'core'=2,'layer'=4] {'z1'..., dimensions={0} | all-to-all | bytes 131072 | tf_op jit(solution)/shard_map/all_to_all | solution.py:36
  77.2 0.0 copy-done
  77.2 3.9 %grafted_products.1 = (f32[128,128]{1,0:T(8,128)}, bf16[128,8,384]{2,1,0:T(8,128)(2,1)S(1)}) custom-call(f32[128,128]{1,0:T(8,128)S(1)} %bitcast.12, f32[128,128]{1,0:T(8,128)S(1)} %copy-done, bf16[128,8,384]{2,1,0:T(8,128)(2,1)S(1)} %all_to_all.25.pieces_ref), custom_call_target="tpu_custom_call" | custom-call | tf_op jit(solution)/shard_map/grafted_products/pallas_call | solution.py:136
  81.1 31.4 %all_to_all.29 = bf16[128,8,384]{2,1,0:T(8,128)(2,1)S(1)} all-to-all(bf16[128,8,384]{2,1,0:T(8,128)(2,1)S(1)} %get-tuple-element.4), channel_id=1, replica_groups=mesh['z4'=2,'z2'=2,'z1'=2,'y4'=2,'y2'=2,'y1'=2,'core'=2,'layer'=4] {'z4'..., dimensions={0} | all-to-all | bytes 1572864 | tf_op jit(solution)/shard_map/all_to_all | solution.py:36
  112.5 0.9 copy.5
  (4 shorter events, 0.0 us)
Async XLA Ops:
  68.2 9.0 %copy-start = (f32[128,128]{1,0:T(8,128)S(1)}, f32[128,128]{1,0:T(8,128)}, u32[]{:S(2)}) copy-start(f32[128,128]{1,0:T(8,128)} %prior_ref.1) | copy-start | bytes 196612

commit v4 on v3

--- a/solution.py
+++ b/solution.py
@@ -23,6 +23,13 @@
 
 def matmul_high(left, right):
     return jnp.dot(left, right, precision=lax.Precision.HIGHEST, preferred_element_type=jnp.float32)
+
+
+def split_three(wide):
+    high = wide.astype(jnp.bfloat16)
+    rest = wide - high.astype(jnp.float32)
+    middle = rest.astype(jnp.bfloat16)
+    return high, middle, (rest - middle.astype(jnp.float32)).astype(jnp.bfloat16)
 
 
 def peers_of(axes):
@@ -103,10 +110,9 @@
         statistic = prior_ref[...] + gram_mean
         held_ref[...] = statistic
         written = pltpu.make_async_copy(held_ref, stat_ref, arrival)
-        written.start()
         ridge = whole_sum(jnp.where(diagonal, statistic, 0.0)) * (ridge_rate / experts)
         shifted = statistic + jnp.where(diagonal, ridge, 0.0)
-        start = 2.5 / jnp.sqrt(whole_sum(shifted * shifted))
+        start = 2.5 * lax.rsqrt(whole_sum(shifted * shifted))
         scaled_identity = jnp.where(diagonal, 1.25, 0.0)
         matrix = start * shifted
         factor = scaled_identity - 0.25 * matrix
@@ -116,9 +122,15 @@
             matrix = matmul_high(matmul_high(square, square), matrix)
             factor = scaled_identity - 0.25 * matrix
             root = matmul_high(root, factor)
+            if repeat == 0:
+                written.start()
         root_bf = root.astype(jnp.bfloat16)
-        root_wide = root_bf.astype(jnp.float32)
-        update_energy = whole_sum(matmul_high(root_wide, gram_mean) * root_wide) / experts
+        root_gram = jnp.dot(
+            jnp.concatenate([root_bf] * 3, axis=1),
+            jnp.concatenate(split_three(gram_mean), axis=0),
+            preferred_element_type=jnp.float32,
+        )
+        update_energy = whole_sum(root_gram * root_bf.astype(jnp.float32)) / experts
         grad_energy = whole_sum(jnp.where(diagonal, gram_mean, 0.0)) / experts
         graft = jnp.sqrt((grad_energy + energy_floor) / (update_energy + energy_floor))
         for row in range(rows):

time: 114 us -> 114 us (level)
  no operation moved by 1% of the time
where the time goes in v4:
time: 114 us; the launch traced here: 113 us
  blocking collectives  107 us (94%)
  Pallas kernels  4.49 us (4%)
    all_to_all x5, blocking collectives, exchanged(): return lax.all_to_all(pieces, axes, split_axis=0, concat_axis=0, tiled=True)  107 us
    pallas_call x1, Pallas kernels, grafted_products(): pl.pallas_call(kernel, out_shape=(pltpu.HBM((experts, experts), jnp.float...  3.86 us

profile of v4, /device:TPU:1, one launch (start us, length us, event | category | flops | bytes accessed | tf_op | source)
XLA Modules:
  0.0 113.4 jit_solution(7621613727986253105)
XLA Ops:
  0.6 44.4 %all_to_all.25.pieces_ref = bf16[128,8,384]{2,1,0:T(8,128)(2,1)S(1)} all-to-all(bf16[128,8,384]{2,1,0:T(8,128)(2,1)} %bitcast.15), channel_id=1, replica_groups=mesh['z4'=2,'z2'=2,'z1'=2,'y4'=2,'y2'=2,'y1'=2,'core'=2,'layer'=4] {'z4'..., dimensions={0} | all-to-all | bytes 1572864 | tf_op jit(solution)/shard_map/all_to_all | solution.py:43
  45.0 0.6 piece_gram.1
  45.6 7.2 %all_to_all.26 = f32[8,16,128]{2,1,0:T(8,128)S(1)} all-to-all(f32[8,16,128]{2,1,0:T(8,128)S(1)} %bitcast.13), channel_id=1, replica_groups=mesh['z4'=2,'z2'=2,'z1'=2,'y4'=2,'y2'=2,'y1'=2,'core'=2,'layer'=4] {'z1'..., dimensions={0} | all-to-all | bytes 131072 | tf_op jit(solution)/shard_map/all_to_all | solution.py:43
  52.8 15.4 %all_to_all.27 = f32[16,16,128]{2,1,0:T(8,128)S(1)} all-to-all(f32[16,16,128]{2,1,0:T(8,128)S(1)} %broadcast_in_dim.4), channel_id=1, replica_groups=mesh['z4'=2,'z2'=2,'z1'=2,'y4'=2,'y2'=2,'y1'=2,'core'=2,'layer'=4] {'z4'..., dimensions={0} | all-to-all | bytes 262144 | tf_op jit(solution)/shard_map/all_to_all | solution.py:43
  68.2 0.0 copy-start
  68.2 8.9 %all_to_all.28 = f32[8,16,128]{2,1,0:T(8,128)S(1)} all-to-all(f32[8,16,128]{2,1,0:T(8,128)S(1)} %broadcast_in_dim.5), channel_id=1, replica_groups=mesh['z4'=2,'z2'=2,'z1'=2,'y4'=2,'y2'=2,'y1'=2,'core'=2,'layer'=4] {'z1'..., dimensions={0} | all-to-all | bytes 131072 | tf_op jit(solution)/shard_map/all_to_all | solution.py:43
  77.2 0.0 copy-done
  77.2 3.9 %grafted_products.1 = (f32[128,128]{1,0:T(8,128)}, bf16[128,8,384]{2,1,0:T(8,128)(2,1)S(1)}) custom-call(f32[128,128]{1,0:T(8,128)S(1)} %bitcast.12, f32[128,128]{1,0:T(8,128)S(1)} %copy-done, bf16[128,8,384]{2,1,0:T(8,128)(2,1)S(1)} %all_to_all.25.pieces_ref), custom_call_target="tpu_custom_call" | custom-call | tf_op jit(solution)/shard_map/grafted_products/pallas_call | solution.py:148
  81.0 31.4 %all_to_all.29 = bf16[128,8,384]{2,1,0:T(8,128)(2,1)S(1)} all-to-all(bf16[128,8,384]{2,1,0:T(8,128)(2,1)S(1)} %get-tuple-element.4), channel_id=1, replica_groups=mesh['z4'=2,'z2'=2,'z1'=2,'y4'=2,'y2'=2,'y1'=2,'core'=2,'layer'=4] {'z4'..., dimensions={0} | all-to-all | bytes 1572864 | tf_op jit(solution)/shard_map/all_to_all | solution.py:43
  112.5 0.9 copy.5
  (4 shorter events, 0.0 us)
Async XLA Ops:
  68.2 9.0 %copy-start = (f32[128,128]{1,0:T(8,128)S(1)}, f32[128,128]{1,0:T(8,128)}, u32[]{:S(2)}) copy-start(f32[128,128]{1,0:T(8,128)} %prior_ref.1) | copy-start | bytes 196612

commit v5 on v4

--- a/solution.py
+++ b/solution.py
@@ -81,29 +81,32 @@
 def piece_gram(pieces):
     experts, rows, width = pieces.shape
 
-    def kernel(pieces_ref, gram_ref, wide_ref):
+    def kernel(pieces_ref, gram_ref, lines_ref, wide_ref):
         widen_rows(pieces_ref, wide_ref)
         gram = jnp.zeros((experts, experts), jnp.float32)
         for row in range(rows):
             line = one_row(wide_ref, row, experts, rows)
+            lines_ref[row] = line
             gram += lax.dot_general(line, line, (((1,), (1,)), ((), ())), preferred_element_type=jnp.float32)
         gram_ref[...] = gram
 
     return pl.pallas_call(
         kernel,
-        out_shape=pltpu.VMEM((experts, experts), jnp.float32),
+        out_shape=(
+            pltpu.VMEM((experts, experts), jnp.float32),
+            pltpu.VMEM((rows, experts, width), jnp.bfloat16),
+        ),
         in_specs=[VMEM],
-        out_specs=VMEM,
+        out_specs=(VMEM,) * 2,
         scratch_shapes=[wide_scratch(experts, rows, width)],
         name="piece_gram",
     )(in_vmem(pieces))
 
 
-def grafted_products(entry_count, gram_sum, prior_stat, pieces):
-    experts, rows, width = pieces.shape
+def grafted_products(entry_count, gram_sum, prior_stat, lines):
+    rows, experts, width = lines.shape
 
-    def kernel(gram_ref, prior_ref, pieces_ref, stat_ref, update_ref, wide_ref, out_ref, held_ref, arrival):
-        widen_rows(pieces_ref, wide_ref)
+    def kernel(gram_ref, prior_ref, lines_ref, stat_ref, update_ref, out_ref, held_ref, arrival):
         shape = (experts, experts)
         diagonal = lax.broadcasted_iota(jnp.int32, shape, 0) == lax.broadcasted_iota(jnp.int32, shape, 1)
         gram_mean = gram_ref[...] * (1.0 / entry_count)
@@ -134,8 +137,7 @@
         grad_energy = whole_sum(jnp.where(diagonal, gram_mean, 0.0)) / experts
         graft = jnp.sqrt((grad_energy + energy_floor) / (update_energy + energy_floor))
         for row in range(rows):
-            line = one_row(wide_ref, row, experts, rows)
-            mixed_bf = jnp.dot(root_bf, line, preferred_element_type=jnp.float32).astype(jnp.bfloat16)
+            mixed_bf = jnp.dot(root_bf, lines_ref[row], preferred_element_type=jnp.float32).astype(jnp.bfloat16)
             update = graft * mixed_bf.astype(jnp.float32)
             for tile in range(width // LANES):
                 out_ref[tile, pl.ds(row, experts, stride=rows), :] = update[:, tile * LANES : (tile + 1) * LANES]
@@ -149,18 +151,17 @@
         kernel,
         out_shape=(
             pltpu.HBM((experts, experts), jnp.float32),
-            pltpu.VMEM(pieces.shape, jnp.bfloat16),
+            pltpu.VMEM((experts, rows, width), jnp.bfloat16),
         ),
         in_specs=[VMEM] * 3,
         out_specs=(pl.BlockSpec(memory_space=pltpu.HBM), VMEM),
         scratch_shapes=[
             wide_scratch(experts, rows, width),
-            wide_scratch(experts, rows, width),
             pltpu.VMEM((experts, experts), jnp.float32),
             pltpu.SemaphoreType.DMA,
         ],
         name="grafted_products",
-    )(in_vmem(gram_sum), in_vmem(prior_stat), in_vmem(pieces))
+    )(in_vmem(gram_sum), in_vmem(prior_stat), in_vmem(lines))
 
 
 def body(gradient, prior_stat):
@@ -171,8 +172,9 @@
     piece = width // columns
     pieces = gradient.reshape(blocks, ROWS, columns, piece).transpose(0, 2, 1, 3).reshape(experts, ROWS, piece)
     regrouped = exchanged(pieces, AXES)
-    gram_sum = summed_over_all(piece_gram(regrouped))
-    statistic, scaled = grafted_products(slab_rows * width, gram_sum, prior_stat, regrouped)
+    gram, lines = piece_gram(regrouped)
+    gram_sum = summed_over_all(gram)
+    statistic, scaled = grafted_products(slab_rows * width, gram_sum, prior_stat, lines)
     returned = exchanged(scaled, AXES)
     update = returned.reshape(blocks, columns, ROWS, piece).transpose(0, 2, 1, 3).reshape(gradient.shape)
     return (update, statistic)

time: 114 us -> 114 us (level)
  no operation moved by 1% of the time
where the time goes in v5:
time: 114 us; the launch traced here: 113 us
  blocking collectives  107 us (94%)
  Pallas kernels  4.48 us (4%)
    all_to_all x5, blocking collectives, exchanged(): return lax.all_to_all(pieces, axes, split_axis=0, concat_axis=0, tiled=True)  107 us
    pallas_call x1, Pallas kernels, grafted_products(): pl.pallas_call(kernel, out_shape=(pltpu.HBM((experts, experts), jnp.float...  3.74 us

profile of v5, /device:TPU:1, one launch (start us, length us, event | category | flops | bytes accessed | tf_op | source)
XLA Modules:
  0.0 113.4 jit_solution(5440887637787853676)
XLA Ops:
  0.6 44.4 %all_to_all.25.pieces_ref = bf16[128,8,384]{2,1,0:T(8,128)(2,1)S(1)} all-to-all(bf16[128,8,384]{2,1,0:T(8,128)(2,1)} %bitcast.15), channel_id=1, replica_groups=mesh['z4'=2,'z2'=2,'z1'=2,'y4'=2,'y2'=2,'y1'=2,'core'=2,'layer'=4] {'z4'..., dimensions={0} | all-to-all | bytes 1572864 | tf_op jit(solution)/shard_map/all_to_all | solution.py:43
  45.0 0.7 piece_gram.1
  45.7 7.2 %all_to_all.26 = f32[8,16,128]{2,1,0:T(8,128)S(1)} all-to-all(f32[8,16,128]{2,1,0:T(8,128)S(1)} %bitcast.13), channel_id=1, replica_groups=mesh['z4'=2,'z2'=2,'z1'=2,'y4'=2,'y2'=2,'y1'=2,'core'=2,'layer'=4] {'z1'..., dimensions={0} | all-to-all | bytes 131072 | tf_op jit(solution)/shard_map/all_to_all | solution.py:43
  52.9 15.3 %all_to_all.27 = f32[16,16,128]{2,1,0:T(8,128)S(1)} all-to-all(f32[16,16,128]{2,1,0:T(8,128)S(1)} %broadcast_in_dim.4), channel_id=1, replica_groups=mesh['z4'=2,'z2'=2,'z1'=2,'y4'=2,'y2'=2,'y1'=2,'core'=2,'layer'=4] {'z4'..., dimensions={0} | all-to-all | bytes 262144 | tf_op jit(solution)/shard_map/all_to_all | solution.py:43
  68.3 0.0 copy-start
  68.3 8.9 %all_to_all.28 = f32[8,16,128]{2,1,0:T(8,128)S(1)} all-to-all(f32[8,16,128]{2,1,0:T(8,128)S(1)} %broadcast_in_dim.5), channel_id=1, replica_groups=mesh['z4'=2,'z2'=2,'z1'=2,'y4'=2,'y2'=2,'y1'=2,'core'=2,'layer'=4] {'z1'..., dimensions={0} | all-to-all | bytes 131072 | tf_op jit(solution)/shard_map/all_to_all | solution.py:43
  77.3 0.0 copy-done
  77.3 3.7 %grafted_products.1 = (f32[128,128]{1,0:T(8,128)}, bf16[128,8,384]{2,1,0:T(8,128)(2,1)S(1)}) custom-call(f32[128,128]{1,0:T(8,128)S(1)} %bitcast.12, f32[128,128]{1,0:T(8,128)S(1)} %copy-done, bf16[8,128,384]{2,1,0:T(8,128)(2,1)S(1)} %get-tuple-element.7.lines_ref), custom_call_target="tpu_custom_call" | custom-call | tf_op jit(solution)/shard_map/grafted_products/pallas_call | solution.py:150
  81.0 31.4 %all_to_all.29 = bf16[128,8,384]{2,1,0:T(8,128)(2,1)S(1)} all-to-all(bf16[128,8,384]{2,1,0:T(8,128)(2,1)S(1)} %get-tuple-element.8), channel_id=1, replica_groups=mesh['z4'=2,'z2'=2,'z1'=2,'y4'=2,'y2'=2,'y1'=2,'core'=2,'layer'=4] {'z4'..., dimensions={0} | all-to-all | bytes 1572864 | tf_op jit(solution)/shard_map/all_to_all | solution.py:43
  112.5 0.9 copy.5
  (4 shorter events, 0.0 us)
Async XLA Ops:
  68.3 9.0 %copy-start = (f32[128,128]{1,0:T(8,128)S(1)}, f32[128,128]{1,0:T(8,128)}, u32[]{:S(2)}) copy-start(f32[128,128]{1,0:T(8,128)} %prior_ref.1) | copy-start | bytes 196612

commit v6 on v5

--- a/solution.py
+++ b/solution.py
@@ -136,11 +136,13 @@
         update_energy = whole_sum(root_gram * root_bf.astype(jnp.float32)) / experts
         grad_energy = whole_sum(jnp.where(diagonal, gram_mean, 0.0)) / experts
         graft = jnp.sqrt((grad_energy + energy_floor) / (update_energy + energy_floor))
-        for row in range(rows):
-            mixed_bf = jnp.dot(root_bf, lines_ref[row], preferred_element_type=jnp.float32).astype(jnp.bfloat16)
+        for row in range(0, rows, 2):
+            pair = jnp.concatenate([lines_ref[row], lines_ref[row + 1]], axis=1)
+            mixed_bf = jnp.dot(root_bf, pair, preferred_element_type=jnp.float32).astype(jnp.bfloat16)
             update = graft * mixed_bf.astype(jnp.float32)
-            for tile in range(width // LANES):
-                out_ref[tile, pl.ds(row, experts, stride=rows), :] = update[:, tile * LANES : (tile + 1) * LANES]
+            for part in range(2 * width // LANES):
+                target = pl.ds(row + part * LANES // width, experts, stride=rows)
+                out_ref[part % (width // LANES), target, :] = update[:, part * LANES : (part + 1) * LANES]
         for tile in range(width // LANES):
             update_ref[:, :, tile * LANES : (tile + 1) * LANES] = (
                 out_ref[tile].reshape(experts, rows, LANES).astype(jnp.bfloat16)

time: 114 us -> 114 us (level)
  no operation moved by 1% of the time
where the time goes in v6:
time: 114 us; the launch traced here: 113 us
  blocking collectives  107 us (94%)
  Pallas kernels  4.46 us (4%)
    all_to_all x5, blocking collectives, exchanged(): return lax.all_to_all(pieces, axes, split_axis=0, concat_axis=0, tiled=True)  107 us
    pallas_call x1, Pallas kernels, grafted_products(): pl.pallas_call(kernel, out_shape=(pltpu.HBM((experts, experts), jnp.float...  3.73 us

profile of v6, /device:TPU:1, one launch (start us, length us, event | category | flops | bytes accessed | tf_op | source)
XLA Modules:
  0.0 113.4 jit_solution(15517894408351566659)
XLA Ops:
  0.6 44.4 %all_to_all.25.pieces_ref = bf16[128,8,384]{2,1,0:T(8,128)(2,1)S(1)} all-to-all(bf16[128,8,384]{2,1,0:T(8,128)(2,1)} %bitcast.15), channel_id=1, replica_groups=mesh['z4'=2,'z2'=2,'z1'=2,'y4'=2,'y2'=2,'y1'=2,'core'=2,'layer'=4] {'z4'..., dimensions={0} | all-to-all | bytes 1572864 | tf_op jit(solution)/shard_map/all_to_all | solution.py:43
  45.0 0.7 piece_gram.1
  45.7 7.2 %all_to_all.26 = f32[8,16,128]{2,1,0:T(8,128)S(1)} all-to-all(f32[8,16,128]{2,1,0:T(8,128)S(1)} %bitcast.13), channel_id=1, replica_groups=mesh['z4'=2,'z2'=2,'z1'=2,'y4'=2,'y2'=2,'y1'=2,'core'=2,'layer'=4] {'z1'..., dimensions={0} | all-to-all | bytes 131072 | tf_op jit(solution)/shard_map/all_to_all | solution.py:43
  52.9 15.3 %all_to_all.27 = f32[16,16,128]{2,1,0:T(8,128)S(1)} all-to-all(f32[16,16,128]{2,1,0:T(8,128)S(1)} %broadcast_in_dim.4), channel_id=1, replica_groups=mesh['z4'=2,'z2'=2,'z1'=2,'y4'=2,'y2'=2,'y1'=2,'core'=2,'layer'=4] {'z4'..., dimensions={0} | all-to-all | bytes 262144 | tf_op jit(solution)/shard_map/all_to_all | solution.py:43
  68.3 0.0 copy-start
  68.3 8.9 %all_to_all.28 = f32[8,16,128]{2,1,0:T(8,128)S(1)} all-to-all(f32[8,16,128]{2,1,0:T(8,128)S(1)} %broadcast_in_dim.5), channel_id=1, replica_groups=mesh['z4'=2,'z2'=2,'z1'=2,'y4'=2,'y2'=2,'y1'=2,'core'=2,'layer'=4] {'z1'..., dimensions={0} | all-to-all | bytes 131072 | tf_op jit(solution)/shard_map/all_to_all | solution.py:43
  77.3 0.0 copy-done
  77.3 3.7 %grafted_products.1 = (f32[128,128]{1,0:T(8,128)}, bf16[128,8,384]{2,1,0:T(8,128)(2,1)S(1)}) custom-call(f32[128,128]{1,0:T(8,128)S(1)} %bitcast.12, f32[128,128]{1,0:T(8,128)S(1)} %copy-done, bf16[8,128,384]{2,1,0:T(8,128)(2,1)S(1)} %get-tuple-element.7.lines_ref), custom_call_target="tpu_custom_call" | custom-call | tf_op jit(solution)/shard_map/grafted_products/pallas_call | solution.py:152
  81.0 31.4 %all_to_all.29 = bf16[128,8,384]{2,1,0:T(8,128)(2,1)S(1)} all-to-all(bf16[128,8,384]{2,1,0:T(8,128)(2,1)S(1)} %get-tuple-element.8), channel_id=1, replica_groups=mesh['z4'=2,'z2'=2,'z1'=2,'y4'=2,'y2'=2,'y1'=2,'core'=2,'layer'=4] {'z4'..., dimensions={0} | all-to-all | bytes 1572864 | tf_op jit(solution)/shard_map/all_to_all | solution.py:43
  112.5 0.9 copy.5
  (4 shorter events, 0.0 us)
Async XLA Ops:
  68.3 9.0 %copy-start = (f32[128,128]{1,0:T(8,128)S(1)}, f32[128,128]{1,0:T(8,128)}, u32[]{:S(2)}) copy-start(f32[128,128]{1,0:T(8,128)} %prior_ref.1) | copy-start | bytes 196612
